TPU v7x, 32 devices: a whole 2x2x4 slice. The times are simulated.
32 devices in a mesh: row: 4 (over z), col: 4 (over x, core), depth: 2 (over y).
Axes of the slice: x: 2, y: 2, z: 4, core: 2. Of those that a mesh axis runs over, the one named last changes fastest.
Arguments:
- heads_concat: bfloat16 [2048, 16384], P('row', ('depth', 'col')), may hold values from -6 to 6
- w_out: bfloat16 [16384, 7168], P(('depth', 'row'), 'col'), may hold values from -0.046875 to 0.046875
Outputs:
- projected: bfloat16 [2048, 7168], P('row', ('col', 'depth'))
All inputs are finite; a program needn't handle non-finite values.
Results may differ from a plain program's by a relative error of at most 0.001.
Values may be sent and summed in bfloat16 or wider, within the bound.
A program may use at most 128 MiB of HBM per device.

v0:
```python
import jax
import jax.numpy as jnp
from jax import lax
from jax.sharding import PartitionSpec as P


def per_device(heads_concat, w_out):
    head_half = lax.all_gather(heads_concat, "col", axis=1, tiled=True)
    weight_half = lax.all_gather(w_out, "row", axis=0, tiled=True)
    partial_sum = jnp.dot(head_half, weight_half, preferred_element_type=jnp.float32)
    summed = lax.psum_scatter(partial_sum, "depth", scatter_dimension=1, tiled=True)
    return summed.astype(jnp.bfloat16)


def solution(mesh):
    return jax.shard_map(
        per_device,
        mesh=mesh,
        in_specs=(P("row", ("depth", "col")), P(("depth", "row"), "col")),
        out_specs=P("row", ("col", "depth")),
        check_vma=False,
    )
```

profile of v0, /device:TPU:0, one launch (start us, length us, event | category | flops | bytes accessed | tf_op | source)
XLA Modules:
  0.0 643.9 jit_solution(13111015978111093550)
XLA Ops:
  6.5 0.0 all-gather.3.cloned.1.call-start
  6.5 0.7 all-gather.3.cloned.1.call-update
  7.3 0.0 all-gather.5.cloned.1.call-start
  7.3 0.7 all-gather.5.cloned.1.call-update
  8.0 0.0 reduce-scatter.2.cloned.1.call-start
  8.1 61.9 %all-gather.3.cloned.1.call-done = bf16[512,8192]{1,0:T(8,128)(2,1)} async-done(((bf16[512,2048]{1,0:T(8,128)(2,1)}), bf16[512,8192]{1,0:T(8,128)(2,1)}) %all-gather.3.cloned.1.call-update) | async-done | bytes 8388624 | tf_op jit(solution)/shard_map/all_gather | solution.py:8
  69.9 494.7 %all-gather.5.cloned.1.call-done = bf16[8192,1792]{1,0:T(8,128)(2,1)} async-done(((bf16[2048,1792]{1,0:T(8,128)(2,1)}), bf16[8192,1792]{1,0:T(8,128)(2,1)}) %all-gather.5.cloned.1.call-update) | async-done | bytes 29360144 | tf_op jit(solution)/shard_map/all_gather | solution.py:9
  564.6 22.7 %fusion = f32[512,1792]{1,0:T(8,128)} fusion(bf16[512,8192]{1,0:T(8,128)(2,1)} %all-gather.3.cloned.1.call-done, bf16[8192,1792]{1,0:T(8,128)(2,1)} %all-gather.5.cloned.1.call-done), kind=kOutput, calls=%fused_computation | convolution fusion | flops 15032385536 | bytes 41418752 | tf_op jit(solution)/shard_map/dot_general | solution.py:10
  587.3 0.0 reduce-scatter.2.cloned.1.call-update
  587.3 47.5 %reduce-scatter.2.cloned.1.call-done = f32[512,896]{1,0:T(8,128)} async-done(((f32[512,1792]{1,0:T(8,128)}), f32[512,896]{1,0:T(8,128)}) %reduce-scatter.2.cloned.1.call-update) | async-done | bytes 1835024 | tf_op jit(solution)/shard_map/reduce_scatter | solution.py:11
  634.9 2.5 convert_element_type.3
Async XLA Ops:
  6.5 63.4 %all-gather.3.cloned.1.call-start = ((), (), s32[]{:S(2)}) async-start(), calls=%async_computation.1 | async-start | bytes 10485760 | tf_op jit(solution)/shard_map/all_gather | solution.py:8
  7.3 557.4 %all-gather.5.cloned.1.call-start = ((), (), s32[]{:S(2)}) async-start(), calls=%async_computation.2 | async-start | bytes 36700160 | tf_op jit(solution)/shard_map/all_gather | solution.py:9
  8.0 626.9 %reduce-scatter.2.cloned.1.call-start = ((), (), s32[]{:S(2)}) async-start(), calls=%async_computation.3 | async-start | bytes 5505024 | tf_op jit(solution)/shard_map/reduce_scatter | solution.py:11
Sparse Core Ops, SparseCore 0:
  8.9 60.9 all-gather.2
  71.5 493.0 all-gather.4
  587.4 47.3 reduce-scatter.1
where the time goes:
time: 644 us
  waiting for transfers between devices  606 us (94%)
  matrix products  22.7 us (4%)
  between operations  13.1 us (2%)
    all_gather x1, waiting for transfers between devices, per_device(): weight_half = lax.all_gather(w_out, 'row', axis=0, tiled=True)  495 us
    all_gather x1, waiting for transfers between devices, per_device(): head_half = lax.all_gather(heads_concat, 'col', axis=1, tiled=True)  61.9 us
    reduce_scatter x1, waiting for transfers between devices, per_device(): lax.psum_scatter(partial_sum, 'depth', scatter_dimension=1, tiled=True)  47.5 us
    dot_general x1, matrix products, per_device(): jnp.dot(head_half, weight_half, preferred_element_type=jnp.float32)  22.7 us
  transfers between devices with their start and end apart: 3, of which 3 were waited for; matrix products, arithmetic and copies ran while one was open for 0% of the time, Pallas kernels for 0%

commit v1 on v0

--- a/solution.py
+++ b/solution.py
@@ -5,7 +5,12 @@
 
 
 def per_device(heads_concat, w_out):
-    head_half = lax.all_gather(heads_concat, "col", axis=1, tiled=True)
+    ring = [heads_concat]
+    for hop in range(3):
+        ring.append(lax.ppermute(ring[-1], "col", [(dev, (dev + 1) % 4) for dev in range(4)]))
+    head_half = jnp.roll(
+        jnp.concatenate(ring[::-1], axis=1), (lax.axis_index("col") + 1) * ring[0].shape[1], axis=1
+    )
     weight_half = lax.all_gather(w_out, "row", axis=0, tiled=True)
     partial_sum = jnp.dot(head_half, weight_half, preferred_element_type=jnp.float32)
     summed = lax.psum_scatter(partial_sum, "depth", scatter_dimension=1, tiled=True)

time: 644 us -> 585 us (0.908)
  waiting for transfers between devices: 606 us -> 523 us
  local copies, waits for them, and re-layouts: 0 us -> 21.7 us
    all_gather x1, waiting for transfers between devices: 495 us -> 398 us  [per_device(): weight_half = lax.all_gather(w_out, 'row', axis=0, tiled=True)]
    ppermute x0 -> x3, waiting for transfers between devices: none -> 77.1 us  [per_device(): lax.ppermute(ring[-1], 'col', [(dev, (dev + 1) % 4) for dev in range(4)])]
    all_gather x1 -> x0, waiting for transfers between devices: 61.9 us -> none  [per_device(): head_half = lax.all_gather(heads_concat, 'col', axis=1, tiled=True)]
    unnamed x0 -> x13, local copies, waits for them, and re-layouts: none -> 20.2 us
  transfers between devices with their start and end apart: 3 -> 5, of which waited for: 3 -> 5; matrix products, arithmetic and copies ran while one was open for 0% -> 3% of each run, Pallas kernels for 0% -> 0%
where the time goes in v1:
time: 585 us; the launch traced here: 584 us
  waiting for transfers between devices  523 us (89%)
  matrix products  22.7 us (4%)
  local copies, waits for them, and re-layouts  21.7 us (4%)
  between operations  13.4 us (2%)
    all_gather x1, waiting for transfers between devices, per_device(): weight_half = lax.all_gather(w_out, 'row', axis=0, tiled=True)  398 us
    ppermute x3, waiting for transfers between devices, per_device(): lax.ppermute(ring[-1], 'col', [(dev, (dev + 1) % 4) for dev in range(4)])  77.1 us
    reduce_scatter x1, waiting for transfers between devices, per_device(): lax.psum_scatter(partial_sum, 'depth', scatter_dimension=1, tiled=True)  47.5 us
    dot_general x1, matrix products, per_device(): jnp.dot(head_half, weight_half, preferred_element_type=jnp.float32)  22.7 us
    unnamed x13, local copies, waits for them, and re-layouts  20.2 us
  transfers between devices with their start and end apart: 5, of which 5 were waited for; matrix products, arithmetic and copies ran while one was open for 3% of the time, Pallas kernels for 0%

profile of v1, /device:TPU:0, one launch (start us, length us, event | category | flops | bytes accessed | tf_op | source)
XLA Modules:
  0.0 584.4 jit_solution(342763510306701381)
XLA Ops:
  6.5 0.0 copy-start
  6.5 0.0 all-gather.2.cloned.1.call-start
  6.5 0.7 all-gather.2.cloned.1.call-update
  7.3 0.0 reduce-scatter.2.cloned.1.call-start
  7.3 0.5 collective-permute-start
  7.8 25.8 %collective-permute-done = bf16[512,2048]{1,0:T(8,128)(2,1)S(1)} collective-permute-done((bf16[512,2048]{1,0:T(8,128)(2,1)}, bf16[512,2048]{1,0:T(8,128)(2,1)S(1)}, u32[]{:S(2)}, u32[]{:S(2)}) %collective-permute-start) | collective-permute-done | bytes 2097184 | tf_op jit(solution)/shard_map/ppermute | solution.py:10
  33.7 0.0 copy-start.1
  33.7 1.4 copy-done.1
  35.0 0.0 collective-permute-start.1
  35.1 25.5 %collective-permute-done.1 = bf16[512,2048]{1,0:T(8,128)(2,1)} collective-permute-done((bf16[512,2048]{1,0:T(8,128)(2,1)S(1)}, bf16[512,2048]{1,0:T(8,128)(2,1)}, u32[]{:S(2)}, u32[]{:S(2)}) %collective-permute-start.1) | collective-permute-done | bytes 2097184 | tf_op jit(solution)/shard_map/ppermute | solution.py:10
  60.6 0.0 collective-permute-start.2
  60.6 0.0 copy-start.2
  60.6 25.8 %collective-permute-done.2 = bf16[512,2048]{1,0:T(8,128)(2,1)} collective-permute-done((bf16[512,2048]{1,0:T(8,128)(2,1)}, bf16[512,2048]{1,0:T(8,128)(2,1)}, u32[]{:S(2)}, u32[]{:S(2)}) %collective-permute-start.2) | collective-permute-done | bytes 2097184 | tf_op jit(solution)/shard_map/ppermute | solution.py:10
  86.4 3.2 constant_dynamic-update-slice_fusion.7
  89.5 3.2 constant_dynamic-update-slice_fusion.6
  92.7 3.2 constant_dynamic-update-slice_fusion.5
  95.9 0.0 copy-done
  95.9 1.5 constant_dynamic-update-slice_fusion.4
  97.5 3.2 constant_dynamic-update-slice_fusion.3
  100.6 3.1 constant_dynamic-update-slice_fusion.2
  103.8 0.0 copy-done.2
  103.8 1.4 constant_dynamic-update-slice_fusion.1
  105.2 1.6 constant_dynamic-update-slice_fusion
  106.8 398.0 %all-gather.2.cloned.1.call-done = bf16[8192,1792]{1,0:T(8,128)(2,1)} async-done(((bf16[2048,1792]{1,0:T(8,128)(2,1)}), bf16[8192,1792]{1,0:T(8,128)(2,1)}) %all-gather.2.cloned.1.call-update) | async-done | bytes 29360144 | tf_op jit(solution)/shard_map/all_gather | solution.py:14
  504.8 22.7 %fusion = f32[512,1792]{1,0:T(8,128)} fusion(bf16[8192,1792]{1,0:T(8,128)(2,1)} %all-gather.2.cloned.1.call-done, bf16[512,16384]{1,0:T(8,128)(2,1)} %constant_dynamic-update-slice_fusion, s32[]{:T(128)S(6)} %select_n.14), kind=kOutput, calls=%fused_computation | convolution fusion | flops 15032385536 | bytes 41418756 | tf_op jit(solution)/shard_map/dot_general | solution.py:15
  527.4 0.0 reduce-scatter.2.cloned.1.call-update
  527.5 47.5 %reduce-scatter.2.cloned.1.call-done = f32[512,896]{1,0:T(8,128)} async-done(((f32[512,1792]{1,0:T(8,128)}), f32[512,896]{1,0:T(8,128)}) %reduce-scatter.2.cloned.1.call-update) | async-done | bytes 1835024 | tf_op jit(solution)/shard_map/reduce_scatter | solution.py:16
  575.0 2.5 convert_element_type.3
Async XLA Ops:
  6.5 89.4 %copy-start = (bf16[512,2048]{1,0:T(8,128)(2,1)S(1)}, bf16[512,2048]{1,0:T(8,128)(2,1)}, u32[]{:S(2)}) copy-start(bf16[512,2048]{1,0:T(8,128)(2,1)} %param.2) | copy-start | bytes 6291460
  6.5 498.2 %all-gather.2.cloned.1.call-start = ((), (), s32[]{:S(2)}) async-start(), calls=%async_computation.1 | async-start | bytes 36700160 | tf_op jit(solution)/shard_map/all_gather | solution.py:14
  7.3 567.7 %reduce-scatter.2.cloned.1.call-start = ((), (), s32[]{:S(2)}) async-start(), calls=%async_computation.2 | async-start | bytes 5505024 | tf_op jit(solution)/shard_map/reduce_scatter | solution.py:16
  7.3 26.4 %collective-permute-start = (bf16[512,2048]{1,0:T(8,128)(2,1)}, bf16[512,2048]{1,0:T(8,128)(2,1)S(1)}, u32[]{:S(2)}, u32[]{:S(2)}) collective-permute-start(bf16[512,2048]{1,0:T(8,128)(2,1)} %param.2), channel_id=1, source_target_pairs={{0,2},{2,4},{4,6},{6,0},{1,3},{3,5},{5,7},{7,1},{8,10},{10,12},{12... | collective-permute-start | bytes 6291464 | tf_op jit(solution)/shard_map/ppermute | solution.py:10
  33.7 1.4 copy-start.1
  35.0 25.6 %collective-permute-start.1 = (bf16[512,2048]{1,0:T(8,128)(2,1)S(1)}, bf16[512,2048]{1,0:T(8,128)(2,1)}, u32[]{:S(2)}, u32[]{:S(2)}) collective-permute-start(bf16[512,2048]{1,0:T(8,128)(2,1)S(1)} %collective-permute-done), channel_id=1, source_target_pairs={{0,2},{2,4},{4,6},{6,0},{1,3},{3,5},{5,7},{7,1},{8,10},{10,12},{12... | collective-permute-start | bytes 6291464 | tf_op jit(solution)/shard_map/ppermute | solution.py:10
  60.6 25.8 %collective-permute-start.2 = (bf16[512,2048]{1,0:T(8,128)(2,1)}, bf16[512,2048]{1,0:T(8,128)(2,1)}, u32[]{:S(2)}, u32[]{:S(2)}) collective-permute-start(bf16[512,2048]{1,0:T(8,128)(2,1)} %collective-permute-done.1), channel_id=1, source_target_pairs={{0,2},{2,4},{4,6},{6,0},{1,3},{3,5},{5,7},{7,1},{8,10},{10,12},{12... | collective-permute-start | bytes 6291464 | tf_op jit(solution)/shard_map/ppermute | solution.py:10
  60.6 43.1 %copy-start.2 = (bf16[512,2048]{1,0:T(8,128)(2,1)S(1)}, bf16[512,2048]{1,0:T(8,128)(2,1)}, u32[]{:S(2)}) copy-start(bf16[512,2048]{1,0:T(8,128)(2,1)} %copy-done.1) | copy-start | bytes 6291460
Sparse Core Ops, SparseCore 0:
  8.9 495.8 all-gather.1
  527.6 47.3 reduce-scatter.1
